TPU v7x, 256 devices: a whole 4x4x8 slice. The times are simulated.
256 devices in a mesh: dp: 32 (over z, x_hi, core), mp: 8 (over x_lo, y).
Axes of the slice: x: 4 (x_hi: 2, x_lo: 2; x = x_hi * 2 + x_lo), y: 4, z: 8, core: 2. Of those that a mesh axis runs over, the one named last changes fastest.
Arguments:
- tokens: bfloat16 [1024, 16384], P('dp', 'mp'), may hold values from -6 to 6
- gate_weight: bfloat16 [16384, 28672], P('mp', 'dp'), may hold values from -0.046875 to 0.046875
- up_weight: bfloat16 [16384, 28672], P('mp', 'dp'), may hold values from -0.046875 to 0.046875
- down_weight: bfloat16 [28672, 16384], P('dp', 'mp'), may hold values from -0.03125 to 0.03125
Outputs:
- mixed: bfloat16 [1024, 16384], P('dp', 'mp')
All inputs are finite; a program needn't handle non-finite values.
Results may differ from a plain program's by a relative error of at most 0.0049.
Values may be sent and summed in bfloat16 or wider, within the bound.
A program may use at most 64 MiB of HBM per device.

v0:
```python
import jax
import jax.numpy as jnp
from jax import lax
from jax.sharding import PartitionSpec as P


def in_order(blocks, dim):
    blocks = jnp.moveaxis(blocks, 0, dim)
    shape = blocks.shape
    return blocks.reshape(*shape[:dim], shape[dim] * shape[dim + 1], *shape[dim + 2 :])


def sent_to_all(x, axis):
    copies = jnp.broadcast_to(x, (lax.axis_size(axis), *x.shape))
    return lax.all_to_all(copies, axis, split_axis=0, concat_axis=0, tiled=True)


def collect(x, axis, dim):
    return in_order(sent_to_all(x, axis), dim)


def per_device(tokens, gate_weight, up_weight, down_weight):
    width = gate_weight.shape[1]
    piece = lax.all_gather(tokens, "dp", axis=0, tiled=True)
    gate_part = jnp.dot(piece, gate_weight, preferred_element_type=jnp.float32)
    up_part = jnp.dot(piece, up_weight, preferred_element_type=jnp.float32)
    partial_both = jnp.concatenate([gate_part, up_part], axis=1)
    share = lax.psum_scatter(partial_both, "mp", scatter_dimension=0, tiled=True)
    own_rows = (jax.nn.silu(share[:, :width]) * share[:, width:]).astype(jnp.bfloat16)
    hidden = collect(own_rows, "mp", 0)
    mixed = lax.psum_scatter(
        jnp.dot(hidden, down_weight, preferred_element_type=jnp.float32),
        "dp",
        scatter_dimension=0,
        tiled=True,
    )
    return mixed.astype(jnp.bfloat16)


def solution(mesh):
    return jax.shard_map(
        per_device,
        mesh=mesh,
        in_specs=(P("dp", "mp"), P("mp", "dp"), P("mp", "dp"), P("dp", "mp")),
        out_specs=P("dp", "mp"),
        check_vma=False,
    )
```

profile of v0, /device:TPU:1, one launch (start us, length us, event | category | flops | bytes accessed | tf_op | source)
XLA Modules:
  0.0 391.3 jit_solution(867062498399786874)
XLA Ops:
  6.5 0.0 all-gather.2.cloned.1.call-start
  6.5 0.7 all-gather.2.cloned.1.call-update
  7.3 0.0 reduce-scatter.3.cloned.1.call-start
  7.3 93.6 %all-gather.2.cloned.1.call-done = bf16[1024,2048]{1,0:T(8,128)(2,1)} async-done(((bf16[32,2048]{1,0:T(8,128)(2,1)}), bf16[1024,2048]{1,0:T(8,128)(2,1)}) %all-gather.2.cloned.1.call-update) | async-done | bytes 4194320 | tf_op jit(solution)/shard_map/all_gather | solution.py:24
  100.9 0.0 copy-start
  100.9 0.0 copy-start.1
  100.9 7.1 %fusion.2 = f32[1024,896]{0,1:T(8,128)S(1)} fusion(bf16[1024,2048]{1,0:T(8,128)(2,1)} %all-gather.2.cloned.1.call-done, bf16[2048,896]{1,0:T(8,128)(2,1)} %param.6), kind=kOutput, calls=%fused_computation.4 | convolution fusion | flops 3758096384 | bytes 11534336 | tf_op jit(solution)/shard_map/dot_general | solution.py:26
  108.0 0.0 copy-done
  108.0 0.0 copy-done.1
  108.0 4.2 %fusion.1 = f32[1024,896]{0,1:T(8,128)S(1)} fusion(bf16[1024,2048]{1,0:T(8,128)(2,1)S(1)} %copy-done, bf16[2048,896]{1,0:T(8,128)(2,1)S(1)} %copy-done.1), kind=kOutput, calls=%fused_computation.3 | convolution fusion | flops 3758096384 | bytes 11534336 | tf_op jit(solution)/shard_map/dot_general | solution.py:25
  112.3 3.7 pad_maximum_fusion
  115.9 0.0 reduce-scatter.3.cloned.1.call-update
  116.0 0.0 reduce-scatter.5.cloned.1.call-start
  116.0 81.8 %reduce-scatter.3.cloned.1.call-done = f32[128,1792]{0,1:T(8,128)} async-done(((f32[1024,1792]{0,1:T(8,128)}), f32[128,1792]{0,1:T(8,128)}) %reduce-scatter.3.cloned.1.call-update) | async-done | bytes 917520 | tf_op jit(solution)/shard_map/reduce_scatter | solution.py:28
  197.8 1.3 fusion
  199.1 0.2 copy.5
  199.2 0.0 copy-start.2
  199.3 0.2 broadcast_in_dim.3
  199.5 25.6 %all_to_all.5 = bf16[8,128,896]{2,1,0:T(8,128)(2,1)S(1)} all-to-all(bf16[8,128,896]{2,1,0:T(8,128)(2,1)S(1)} %broadcast_in_dim.3), channel_id=1, replica_groups=mesh['dp'=32,'mp'=8] {'mp'}, dimensions={0} | all-to-all | bytes 3670016 | tf_op jit(solution)/shard_map/all_to_all | solution.py:15
  225.1 0.0 copy-done.2
  225.1 6.8 %fusion.3 = f32[1024,2048]{1,0:T(8,128)} fusion(bf16[1024,896]{1,0:T(8,128)(2,1)S(1)} %bitcast.7, bf16[896,2048]{1,0:T(8,128)(2,1)S(1)} %copy-done.2), kind=kOutput, calls=%fused_computation.5 | convolution fusion | flops 3758096384 | bytes 13893632 | tf_op jit(solution)/shard_map/dot_general | solution.py:32
  231.9 0.0 reduce-scatter.5.cloned.1.call-update
  231.9 151.3 %reduce-scatter.5.cloned.1.call-done = f32[32,2048]{1,0:T(8,128)} async-done(((f32[1024,2048]{1,0:T(8,128)}), f32[32,2048]{1,0:T(8,128)}) %reduce-scatter.5.cloned.1.call-update) | async-done | bytes 262160 | tf_op jit(solution)/shard_map/reduce_scatter | solution.py:31
  383.2 1.6 convert_element_type.7
Async XLA Ops:
  6.5 94.4 %all-gather.2.cloned.1.call-start = ((), (), s32[]{:S(2)}) async-start(), calls=%async_computation.3 | async-start | bytes 4325376 | tf_op jit(solution)/shard_map/all_gather | solution.py:24
  7.3 190.5 %reduce-scatter.3.cloned.1.call-start = ((), (), s32[]{:S(2)}) async-start(), calls=%async_computation.4 | async-start | bytes 8257536 | tf_op jit(solution)/shard_map/reduce_scatter | solution.py:28
  100.9 7.1 %copy-start = (bf16[1024,2048]{1,0:T(8,128)(2,1)S(1)}, bf16[1024,2048]{1,0:T(8,128)(2,1)}, u32[]{:S(2)}) copy-start(bf16[1024,2048]{1,0:T(8,128)(2,1)} %all-gather.2.cloned.1.call-done) | copy-start | bytes 12582916
  100.9 7.1 %copy-start.1 = (bf16[2048,896]{1,0:T(8,128)(2,1)S(1)}, bf16[2048,896]{1,0:T(8,128)(2,1)}, u32[]{:S(2)}) copy-start(bf16[2048,896]{1,0:T(8,128)(2,1)} %param.5) | copy-start | bytes 11010052
  116.0 267.2 %reduce-scatter.5.cloned.1.call-start = ((), (), s32[]{:S(2)}) async-start(), calls=%async_computation.5 | async-start | bytes 8650752 | tf_op jit(solution)/shard_map/reduce_scatter | solution.py:31
  199.2 25.9 %copy-start.2 = (bf16[896,2048]{1,0:T(8,128)(2,1)S(1)}, bf16[896,2048]{1,0:T(8,128)(2,1)}, u32[]{:S(2)}) copy-start(bf16[896,2048]{1,0:T(8,128)(2,1)} %param.7) | copy-start | bytes 11010052
Sparse Core Ops, SparseCore 0:
  10.1 90.7 all-gather.1
  116.1 81.6 reduce-scatter.2
  232.0 151.1 reduce-scatter.4
where the time goes:
time: 395 us; the launch traced here: 391 us
  waiting for transfers between devices  327 us (83%)
  blocking collectives  25.6 us (6%)
  matrix products  18.1 us (5%)
  between operations  13.2 us (3%)
  other arithmetic  6.57 us (2%)
    reduce_scatter x1, waiting for transfers between devices, per_device(): lax.psum_scatter(jnp.dot(hidden, down_weight, preferred_element_type=jnp....  151 us
    all_gather x1, waiting for transfers between devices, per_device(): piece = lax.all_gather(tokens, 'dp', axis=0, tiled=True)  93.6 us
    reduce_scatter x1, waiting for transfers between devices, per_device(): lax.psum_scatter(partial_both, 'mp', scatter_dimension=0, tiled=True)  81.8 us
    all_to_all x1, blocking collectives, sent_to_all(): return lax.all_to_all(copies, axis, split_axis=0, concat_axis=0, tiled=True)  25.6 us
  transfers between devices with their start and end apart: 3, of which 3 were waited for; matrix products, arithmetic and copies ran while one was open for 0% of the time, Pallas kernels for 0%

commit v1 on v0

v1 whole, which is shorter than its diff:
```python
import jax
import jax.numpy as jnp
from jax import lax
from jax.experimental import pallas as pl
from jax.experimental.pallas import tpu as pltpu
from jax.sharding import PartitionSpec as P

MESH = pl.DeviceIdType.MESH
BF16, F32 = jnp.bfloat16, jnp.float32
SLABS = 8
PLAN = (
    ("gate_up", 1),
    ("add_y", 2),
    ("spread_y", 3),
    ("down", 4),
    ("send_z", 5),
    ("relay_y", 1),
    ("activate", 2),
    ("to_twin", 3),
)
HOP_TICKS = (0, 1, 3, 4, 5)

COPIES = dict(
    pair=1, up_ring=4, down_ring=4, twin_in=8,
    far=16, direct=16, joint=16, cross=8, cross_h=8, spread=24, twin_h=8,
    half=8, home=8, out=1, weight=1,
)
BASE, TOTAL = {}, 0
for _name, _count in COPIES.items():
    BASE[_name], TOTAL = TOTAL, TOTAL + _count


def kernel(tokens, gate_w, up_w, down_w, out, T, GU, DW, PG, FS, FR, SS, SR, YB, XR, HB, PO, XS, XD, ZS, ZR, FIN, OS, OR, local, sent, got):
    dp, mp = lax.axis_index("dp"), lax.axis_index("mp")
    z, xh, c = dp // 4, (dp // 2) & 1, dp & 1
    xl, y = mp // 4, mp & 3
    width = gate_w.shape[1]
    half = DW.shape[2]

    def device(z_=z, xh_=xh, c_=c, xl_=xl, y_=y):
        return (z_ * 4 + xh_ * 2 + c_, xl_ * 4 + y_)

    twin = device(c_=1 - c)
    pair = device(xh_=1 - xh)
    cross = device(xl_=1 - xl)
    y_up, y_down, y_far = (device(y_=(y + n) & 3) for n in (1, 3, 2))

    def at_z(n):
        return device(z_=(z + n) & 7)

    mine = pl.multiple_of(c * half, half)
    other = pl.multiple_of((1 - c) * half, half)
    loads = [
        pltpu.make_async_copy(tokens, T.at[z, 2 * c + xh], local.at[0]),
        pltpu.make_async_copy(gate_w, GU.at[:, pl.ds(0, width)], local.at[1]),
        pltpu.make_async_copy(up_w, GU.at[:, pl.ds(width, width)], local.at[2]),
        pltpu.make_async_copy(down_w.at[:, pl.ds(mine, half)], DW.at[c], local.at[3]),
    ]
    for load in loads:
        load.start()

    barrier = pltpu.get_barrier_semaphore()
    friends = [twin, pair, cross, y_up, y_down, y_far] + [at_z(n) for n in range(1, 8)]
    for friend in friends:
        pl.semaphore_signal(barrier, inc=1, device_id=friend, device_id_type=MESH)
    pl.semaphore_wait(barrier, len(friends))

    def copy(name, n, src, dst, to, lands=None):
        return pltpu.make_async_remote_copy(
            src_ref=src,
            dst_ref=dst,
            send_sem=sent.at[BASE[name] + n],
            recv_sem=got.at[BASE[name] + (n if lands is None else lands)],
            device_id=to,
            device_id_type=MESH,
        )

    def slab(n):
        return (z + n) & 7

    def ring_piece(n):
        return T.at[slab(n), pl.ds(2 * c, 2)]

    def ring_half(n, side):
        return T.at[slab(n), pl.ds(2 * c, 2), :, pl.ds(side * half, half)]

    def ring_down(hop):
        ref = ring_piece(hop) if hop < 3 else ring_half(hop, 0)
        return copy("down_ring", hop, ref, ref, at_z(7))

    def ring_up(hop):
        ref = ring_piece(-hop) if hop < 3 else ring_half(-hop, 1)
        return copy("up_ring", hop, ref, ref, at_z(1))

    def from_above(hop):
        ref = ring_piece(hop + 1) if hop < 3 else ring_half(hop + 1, 0)
        return copy("down_ring", hop, ref, ref, at_z(1))

    def from_below(hop):
        ref = ring_piece(-hop - 1) if hop < 3 else ring_half(-hop - 1, 1)
        return copy("up_ring", hop, ref, ref, at_z(7))

    def twin_in(n, core):
        ref = T.at[slab(n), pl.ds(2 * core, 2)]
        return copy("twin_in", n & 7, ref, ref, twin)

    def pair_in(half_):
        ref = T.at[z, 2 * c + half_]
        return copy("pair", 0, ref, ref, pair)

    weight_out = copy("weight", 0, down_w.at[:, pl.ds(other, half)], DW.at[c], twin)
    weight_in = copy("weight", 0, DW.at[1 - c], DW.at[1 - c], twin)

    def hop(n):
        if n == 0:
            loads[0].wait()
            pair_in(xh).start()
            pair_in(1 - xh).wait_recv()
            ring_down(0).start()
            ring_up(0).start()
            twin_in(0, c).start()
            weight_out.start()
            return
        from_above(n - 1).wait_recv()
        from_below(n - 1).wait_recv()
        if n < 4:
            ring_down(n).start()
            ring_up(n).start()
            twin_in(n, c).start()
            twin_in(-n, c).start()
        else:
            twin_in(4, c).start()

    def place(k):
        return jnp.where(k == 2, 7, jnp.where(k < 2, k, k - 1))

    def far(k, g):
        return copy("far", 2 * k + g, FS.at[k, g], FR.at[k, g], y_down if g else y_up)

    def joint(k, g):
        return copy("joint", 2 * k + g, SS.at[k, g], SR.at[k, g], y_down if g else y_up)

    def direct(k, g):
        return copy("direct", 2 * k + g, SS.at[k, 2 + g], SR.at[k, 2 + g], y_up if g else y_down)

    def cross_sum(k):
        return copy("cross", k, YB.at[k, 1 - xl], XR.at[k], cross)

    def cross_h(k, x):
        ref = HB.at[k, c, y, x]
        return copy("cross_h", k, ref, ref, cross)

    def spread(k, n, row, to):
        ref = HB.at[k, c, row]
        return copy("spread", 3 * k + n, ref, ref, to)

    def spreads(k):
        return [spread(k, n, y, to) for n, to in enumerate((y_up, y_down, y_far))]

    def spread_in(k):
        return [spread(k, n, (y + m) & 3, y_far) for n, m in enumerate((3, 1, 2))]

    def twin_h(k, core):
        ref = HB.at[k, core]
        return copy("twin_h", k, ref, ref, twin)

    def halves(k):
        return copy("half", k, XS.at[k], XD.at[k], pair)

    def home(k):
        return copy("home", k, ZS.at[k], ZR.at[k], at_z(place(k)))

    def gate_up(k):
        n = place(k)
        s = slab(n)
        twin_in(n, 1 - c).wait_recv()

        @pl.when(k == 0)
        def _():
            loads[1].wait()
            loads[2].wait()

        @pl.loop(0, 7)
        def _(i):
            columns = pl.ds(pl.multiple_of(i * 256, 256), 256)
            rows = jnp.concatenate([T[s, (y + m) & 3] for m in (2, 1, 3, 0)], axis=0)
            PG[k, :, columns] = jnp.dot(rows, GU[:, columns], preferred_element_type=F32)

        FS[k, 0] = PG[k, 0:32, 0:width].astype(BF16)
        FS[k, 1] = PG[k, 0:32, width:].astype(BF16)
        far(k, 0).start()
        far(k, 1).start()
        SS[k, 2] = PG[k, 64:96, 0:width].astype(BF16)
        SS[k, 3] = PG[k, 32:64, width:].astype(BF16)
        direct(k, 0).start()
        direct(k, 1).start()

    def relay_y(k):
        far(k, 0).wait_recv()
        far(k, 1).wait_recv()
        SS[k, 0] = (PG[k, 32:64, 0:width] + FR[k, 0].astype(F32)).astype(BF16)
        SS[k, 1] = (PG[k, 64:96, width:] + FR[k, 1].astype(F32)).astype(BF16)
        joint(k, 0).start()
        joint(k, 1).start()

    def add_y(k):
        for g in (0, 1):
            joint(k, g).wait_recv()
            direct(k, g).wait_recv()
        for g in (0, 1):
            total = PG[k, 96:128, g * width : (g + 1) * width] + (SR[k, g].astype(F32) + SR[k, 2 + g].astype(F32))
            YB[k, 0, g] = total[0:16]
            YB[k, 1, g] = total[16:32]
        cross_sum(k).start()

    def activate(k):
        cross_sum(k).wait_recv()
        gate = YB[k, xl, 0] + XR[k, 0]
        up = YB[k, xl, 1] + XR[k, 1]
        HB[k, c, y, xl] = (gate / (1 + jnp.exp(-gate)) * up).astype(BF16)
        cross_h(k, xl).start()

    def spread_y(k):
        cross_h(k, 1 - xl).wait_recv()
        for send in spreads(k):
            send.start()

    def to_twin(k):
        for piece in spread_in(k):
            piece.wait_recv()
        twin_h(k, c).start()

    def down(k):
        twin_h(k, 1 - c).wait_recv()

        @pl.when(k == 0)
        def _():
            loads[3].wait()
            weight_in.wait_recv()

        @pl.loop(0, half // 256)
        def _(i):
            columns = pl.ds(pl.multiple_of(i * 256, 256), 256)
            own = jnp.dot(HB[k, 0].reshape(128, width), DW[0, :, columns], preferred_element_type=F32)
            total = own + jnp.dot(HB[k, 1].reshape(128, width), DW[1, :, columns], preferred_element_type=F32)
            PO[k, :, :, columns] = total.reshape(4, 32, 256)

        XS[k, 0] = PO[k, 1 - xh].astype(BF16)
        XS[k, 1] = PO[k, 3 - xh].astype(BF16)
        halves(k).start()

    def send_z(k):
        halves(k).wait_recv()
        totals = [PO[k, 2 * core + xh] + XD[k, core].astype(F32) for core in (0, 1)]

        @pl.when(k == 0)
        def _():
            FIN[0] = totals[0]
            FIN[1] = totals[1]

        @pl.when(k > 0)
        def _():
            ZS[k, 0] = totals[0].astype(BF16)
            ZS[k, 1] = totals[1].astype(BF16)
            home(k).start()

    stages = dict(gate_up=gate_up, relay_y=relay_y, add_y=add_y, activate=activate, spread_y=spread_y, to_twin=to_twin, down=down, send_z=send_z)

    def tick(i, carry):
        for name, lag in PLAN:

            @pl.when((i >= lag) & (i < lag + SLABS))
            def _():
                stages[name](i - lag)

        for n, when in enumerate(HOP_TICKS):

            @pl.when(i == when)
            def _():
                hop(n)

        return carry

    lax.fori_loop(0, SLABS + max(lag for _, lag in PLAN), tick, 0)

    for k in range(1, SLABS):
        home(k).wait_recv()
    out_copy = copy("out", 0, OS, OR, twin)
    for core in (0, 1):
        total = FIN[core]
        for k in range(1, SLABS):
            total += ZR[k, core].astype(F32)
        FIN[core] = total
    OS[...] = FIN[1 - c].astype(BF16)
    out_copy.start()
    out[:, pl.ds(mine, half)] = FIN[c].astype(BF16)
    out_copy.wait_recv()
    out[:, pl.ds(other, half)] = OR[...]

    pair_in(xh).wait_send()
    weight_out.wait_send()
    out_copy.wait_send()
    for n in range(4):
        ring_down(n).wait_send()
        ring_up(n).wait_send()

    def drain(k, carry):
        twin_in(k, c).wait_send()
        for g in (0, 1):
            far(k, g).wait_send()
            direct(k, g).wait_send()
            joint(k, g).wait_send()
        cross_sum(k).wait_send()
        cross_h(k, xl).wait_send()
        for send in spreads(k):
            send.wait_send()
        twin_h(k, c).wait_send()
        halves(k).wait_send()

        @pl.when(k > 0)
        def _():
            home(k).wait_send()

        return carry

    lax.fori_loop(0, SLABS, drain, 0)


def per_device(tokens, gate_weight, up_weight, down_weight):
    rows, depth = tokens.shape
    width = gate_weight.shape[1]
    half = down_weight.shape[1] // 2
    dma = pltpu.SemaphoreType.DMA
    return pl.pallas_call(
        kernel,
        out_shape=jax.ShapeDtypeStruct((rows, 2 * half), BF16),
        in_specs=[pl.BlockSpec(memory_space=pl.ANY)] * 4,
        out_specs=pl.BlockSpec(memory_space=pltpu.VMEM),
        scratch_shapes=[
            pltpu.VMEM((8, 4, rows, depth), BF16),
            pltpu.VMEM((depth, 2 * width), BF16),
            pltpu.VMEM((2, width, half), BF16),
            pltpu.VMEM((8, 128, 2 * width), F32),
            pltpu.VMEM((8, 2, 32, width), BF16),
            pltpu.VMEM((8, 2, 32, width), BF16),
            pltpu.VMEM((8, 4, 32, width), BF16),
            pltpu.VMEM((8, 4, 32, width), BF16),
            pltpu.VMEM((8, 2, 2, 16, width), F32),
            pltpu.VMEM((8, 2, 16, width), F32),
            pltpu.VMEM((8, 2, 4, 2, 16, width), BF16),
            pltpu.VMEM((8, 4, 32, half), F32),
            pltpu.VMEM((8, 2, 32, half), BF16),
            pltpu.VMEM((8, 2, 32, half), BF16),
            pltpu.VMEM((8, 2, 32, half), BF16),
            pltpu.VMEM((8, 2, 32, half), BF16),
            pltpu.VMEM((2, 32, half), F32),
            pltpu.VMEM((32, half), BF16),
            pltpu.VMEM((32, half), BF16),
            dma((4,)),
            dma((TOTAL,)),
            dma((TOTAL,)),
        ],
        compiler_params=pltpu.CompilerParams(collective_id=0, has_side_effects=True, vmem_limit_bytes=67043328),
        name="block",
    )(tokens, gate_weight, up_weight, down_weight)


def solution(mesh):
    return jax.shard_map(
        per_device,
        mesh=mesh,
        in_specs=(P("dp", "mp"), P("mp", "dp"), P("mp", "dp"), P("dp", "mp")),
        out_specs=P("dp", "mp"),
        check_vma=False,
    )
```

time: 395 us -> 131 us (0.33)
  waiting for transfers between devices: 327 us -> 0 us
  Pallas kernels: 0 us -> 128 us
  blocking collectives: 25.6 us -> 0 us
  matrix products: 18.1 us -> 0 us
  between operations: 13.2 us -> 0.01 us
  other arithmetic: 6.57 us -> 0 us
    reduce_scatter x2 -> x0, waiting for transfers between devices: 233 us -> none  [the longest x1 151 us: per_device(): lax.psum_scatter(jnp.dot(hidden, down_weight, preferred_element_type=jnp....]
    pallas_call x0 -> x1, Pallas kernels: none -> 128 us  [per_device(): pl.pallas_call(kernel, out_shape=jax.ShapeDtypeStruct((rows, 2 * half), B...]
    all_gather x1 -> x0, waiting for transfers between devices: 93.6 us -> none  [per_device(): piece = lax.all_gather(tokens, 'dp', axis=0, tiled=True)]
    all_to_all x1 -> x0, blocking collectives: 25.6 us -> none  [sent_to_all(): return lax.all_to_all(copies, axis, split_axis=0, concat_axis=0, tiled=True)]
    dot_general x3 -> x0, matrix products: 18.1 us -> none  [the longest x1 7.06 us: per_device(): up_part = jnp.dot(piece, up_weight, preferred_element_type=jnp.float32)]
  transfers between devices with their start and end apart: 3 -> 0, of which waited for: 3 -> 0; matrix products, arithmetic and copies ran while one was open for 0% -> 0% of each run, Pallas kernels for 0% -> 0%
where the time goes in v1:
time: 131 us; the launch traced here: 130 us
  Pallas kernels  128 us (98%)
  local copies, waits for them, and re-layouts  1.57 us (1%)
    pallas_call x1, Pallas kernels, per_device(): pl.pallas_call(kernel, out_shape=jax.ShapeDtypeStruct((rows, 2 * half), B...  128 us

profile of v1, /device:TPU:1, one launch (start us, length us, event | category | flops | bytes accessed | tf_op | source)
XLA Modules:
  0.0 130.0 jit_solution(2287708490743885401)
XLA Ops:
  0.0 128.4 %block.1 = bf16[32,2048]{1,0:T(8,128)(2,1)} custom-call(bf16[32,2048]{1,0:T(8,128)(2,1)} %tokens.1, bf16[2048,896]{1,0:T(8,128)(2,1)} %gate_w.1, bf16[2048,896]{1,0:T(8,128)(2,1)} %up_w.1, bf16[896,2048]{1,0:T(8,128)(2,1)} %down_w.1), custom_call_target="tpu_custom_call" | custom-call | tf_op jit(solution)/shard_map/block/pallas_call | solution.py:334
  128.4 1.6 %copy.6 = bf16[32,2048]{1,0:T(8,128)(2,1)} copy(bf16[32,2048]{1,0:T(8,128)(2,1)} %block.1) | data formatting | bytes 262144

commit v2 on v1

--- a/solution.py
+++ b/solution.py
@@ -5,23 +5,29 @@
 from jax.experimental.pallas import tpu as pltpu
 from jax.sharding import PartitionSpec as P
 
+
+def arrive(copy):
+    with jax.named_scope("wait"):
+        copy.wait_recv()
+
 MESH = pl.DeviceIdType.MESH
 BF16, F32 = jnp.bfloat16, jnp.float32
 SLABS = 8
-PLAN = (
-    ("gate_up", 1),
-    ("add_y", 2),
-    ("spread_y", 3),
-    ("down", 4),
-    ("send_z", 5),
-    ("relay_y", 1),
-    ("activate", 2),
-    ("to_twin", 3),
+PLACE = (0, 1, 2, 3, 4, 5, 6, 7)
+STAGES = dict(g="gate_up", r="relay_y", a="add_y", s="activate", p="spread_y", t="to_twin", d="down", z="send_z")
+ORDER = (
+    "h00", "h01", "h10", "g0", "h11", "r0", "h20", "g1", "h21", "g7", "g6", "a0",
+    "h30", "h31", "r1", "g2", "g3", "a1", "h40", "s0", "r6", "r2", "r3", "g4",
+    "a6", "g5", "s1", "a3", "r4", "s6", "a2", "r5", "r7", "s3", "a4", "p6",
+    "s2", "a5", "p3", "s4", "p0", "t6", "a7", "p4", "p1", "t3", "s5", "d6",
+    "d3", "t0", "p5", "p2", "t4", "s7", "z6", "d4", "t5", "z3", "p7", "t2",
+    "d5", "z4", "t1", "d2", "t7", "d1", "z5", "d7", "d0", "z2", "z1", "z7",
+    "z0",
 )
-HOP_TICKS = (0, 1, 3, 4, 5)
+FIRST_DOWN = next(step for step in ORDER if step[0] == "d")
 
 COPIES = dict(
-    pair=1, up_ring=4, down_ring=4, twin_in=8,
+    pair=1, up_ring=8, down_ring=8, twin_in=16,
     far=16, direct=16, joint=16, cross=8, cross_h=8, spread=24, twin_h=8,
     half=8, home=8, out=1, weight=1,
 )
@@ -78,61 +84,63 @@
     def slab(n):
         return (z + n) & 7
 
-    def ring_piece(n):
-        return T.at[slab(n), pl.ds(2 * c, 2)]
-
-    def ring_half(n, side):
-        return T.at[slab(n), pl.ds(2 * c, 2), :, pl.ds(side * half, half)]
-
-    def ring_down(hop):
-        ref = ring_piece(hop) if hop < 3 else ring_half(hop, 0)
-        return copy("down_ring", hop, ref, ref, at_z(7))
-
-    def ring_up(hop):
-        ref = ring_piece(-hop) if hop < 3 else ring_half(-hop, 1)
-        return copy("up_ring", hop, ref, ref, at_z(1))
-
-    def from_above(hop):
-        ref = ring_piece(hop + 1) if hop < 3 else ring_half(hop + 1, 0)
-        return copy("down_ring", hop, ref, ref, at_z(1))
-
-    def from_below(hop):
-        ref = ring_piece(-hop - 1) if hop < 3 else ring_half(-hop - 1, 1)
-        return copy("up_ring", hop, ref, ref, at_z(7))
-
-    def twin_in(n, core):
-        ref = T.at[slab(n), pl.ds(2 * core, 2)]
-        return copy("twin_in", n & 7, ref, ref, twin)
-
-    def pair_in(half_):
-        ref = T.at[z, 2 * c + half_]
+    def piece(n, part, core):
+        return T.at[slab(n), 2 * core + (1 - xh if part else xh)]
+
+    def ring_down(hop, part):
+        ref = piece(hop, part, c)
+        return copy("down_ring", 2 * hop + part, ref, ref, at_z(7))
+
+    def ring_up(hop, part):
+        ref = piece(-hop, part, c)
+        return copy("up_ring", 2 * hop + part, ref, ref, at_z(1))
+
+    def from_above(hop, part):
+        ref = piece(hop + 1, part, c)
+        return copy("down_ring", 2 * hop + part, ref, ref, at_z(1))
+
+    def from_below(hop, part):
+        ref = piece(-hop - 1, part, c)
+        return copy("up_ring", 2 * hop + part, ref, ref, at_z(7))
+
+    def twin_in(n, part, core):
+        row = 1 - xh if part else xh
+        ref = T.at[slab(n), 2 * core + row]
+        return copy("twin_in", 2 * (n % 8) + part, ref, ref, twin)
+
+    def pair_in(part):
+        ref = piece(0, part, c)
         return copy("pair", 0, ref, ref, pair)
 
     weight_out = copy("weight", 0, down_w.at[:, pl.ds(other, half)], DW.at[c], twin)
     weight_in = copy("weight", 0, DW.at[1 - c], DW.at[1 - c], twin)
 
-    def hop(n):
+    def hop(n, part):
         if n == 0:
-            loads[0].wait()
-            pair_in(xh).start()
-            pair_in(1 - xh).wait_recv()
-            ring_down(0).start()
-            ring_up(0).start()
-            twin_in(0, c).start()
-            weight_out.start()
-            return
-        from_above(n - 1).wait_recv()
-        from_below(n - 1).wait_recv()
-        if n < 4:
-            ring_down(n).start()
-            ring_up(n).start()
-            twin_in(n, c).start()
-            twin_in(-n, c).start()
+            if part == 0:
+                loads[0].wait()
+                pair_in(0).start()
+            else:
+                arrive(pair_in(1))
+            ring_down(0, part).start()
+            ring_up(0, part).start()
+            twin_in(0, part, c).start()
+            if part == 1:
+                weight_out.start()
+        elif n < 4:
+            arrive(from_above(n - 1, part))
+            arrive(from_below(n - 1, part))
+            if n < 3 or part == 0:
+                ring_down(n, part).start()
+            if n < 3 or part == 1:
+                ring_up(n, part).start()
+            twin_in(n, part, c).start()
+            twin_in(-n, part, c).start()
         else:
-            twin_in(4, c).start()
-
-    def place(k):
-        return jnp.where(k == 2, 7, jnp.where(k < 2, k, k - 1))
+            arrive(from_above(3, 0))
+            arrive(from_below(3, 1))
+            twin_in(4, 0, c).start()
+            twin_in(4, 1, c).start()
 
     def far(k, g):
         return copy("far", 2 * k + g, FS.at[k, g], FR.at[k, g], y_down if g else y_up)
@@ -168,15 +176,14 @@
         return copy("half", k, XS.at[k], XD.at[k], pair)
 
     def home(k):
-        return copy("home", k, ZS.at[k], ZR.at[k], at_z(place(k)))
+        return copy("home", k, ZS.at[k], ZR.at[k], at_z(PLACE[k]))
 
     def gate_up(k):
-        n = place(k)
+        n = PLACE[k]
         s = slab(n)
-        twin_in(n, 1 - c).wait_recv()
-
-        @pl.when(k == 0)
-        def _():
+        arrive(twin_in(n, 0, 1 - c))
+        arrive(twin_in(n, 1, 1 - c))
+        if k == 0:
             loads[1].wait()
             loads[2].wait()
 
@@ -196,8 +203,8 @@
         direct(k, 1).start()
 
     def relay_y(k):
-        far(k, 0).wait_recv()
-        far(k, 1).wait_recv()
+        arrive(far(k, 0))
+        arrive(far(k, 1))
         SS[k, 0] = (PG[k, 32:64, 0:width] + FR[k, 0].astype(F32)).astype(BF16)
         SS[k, 1] = (PG[k, 64:96, width:] + FR[k, 1].astype(F32)).astype(BF16)
         joint(k, 0).start()
@@ -205,8 +212,8 @@
 
     def add_y(k):
         for g in (0, 1):
-            joint(k, g).wait_recv()
-            direct(k, g).wait_recv()
+            arrive(joint(k, g))
+            arrive(direct(k, g))
         for g in (0, 1):
             total = PG[k, 96:128, g * width : (g + 1) * width] + (SR[k, g].astype(F32) + SR[k, 2 + g].astype(F32))
             YB[k, 0, g] = total[0:16]
@@ -214,29 +221,28 @@
         cross_sum(k).start()
 
     def activate(k):
-        cross_sum(k).wait_recv()
+        arrive(cross_sum(k))
         gate = YB[k, xl, 0] + XR[k, 0]
         up = YB[k, xl, 1] + XR[k, 1]
         HB[k, c, y, xl] = (gate / (1 + jnp.exp(-gate)) * up).astype(BF16)
         cross_h(k, xl).start()
 
     def spread_y(k):
-        cross_h(k, 1 - xl).wait_recv()
+        arrive(cross_h(k, 1 - xl))
         for send in spreads(k):
             send.start()
 
     def to_twin(k):
         for piece in spread_in(k):
-            piece.wait_recv()
+            arrive(piece)
         twin_h(k, c).start()
 
     def down(k):
-        twin_h(k, 1 - c).wait_recv()
-
-        @pl.when(k == 0)
-        def _():
+        arrive(twin_h(k, 1 - c))
+
+        if "d%d" % k == FIRST_DOWN:
             loads[3].wait()
-            weight_in.wait_recv()
+            arrive(weight_in)
 
         @pl.loop(0, half // 256)
         def _(i):
@@ -250,41 +256,29 @@
         halves(k).start()
 
     def send_z(k):
-        halves(k).wait_recv()
+        arrive(halves(k))
         totals = [PO[k, 2 * core + xh] + XD[k, core].astype(F32) for core in (0, 1)]
 
-        @pl.when(k == 0)
-        def _():
+        if k == 0:
             FIN[0] = totals[0]
             FIN[1] = totals[1]
-
-        @pl.when(k > 0)
-        def _():
+        else:
             ZS[k, 0] = totals[0].astype(BF16)
             ZS[k, 1] = totals[1].astype(BF16)
             home(k).start()
 
     stages = dict(gate_up=gate_up, relay_y=relay_y, add_y=add_y, activate=activate, spread_y=spread_y, to_twin=to_twin, down=down, send_z=send_z)
 
-    def tick(i, carry):
-        for name, lag in PLAN:
-
-            @pl.when((i >= lag) & (i < lag + SLABS))
-            def _():
-                stages[name](i - lag)
-
-        for n, when in enumerate(HOP_TICKS):
-
-            @pl.when(i == when)
-            def _():
-                hop(n)
-
-        return carry
-
-    lax.fori_loop(0, SLABS + max(lag for _, lag in PLAN), tick, 0)
+    for step in ORDER:
+        if step[0] == "h":
+            with jax.named_scope(step):
+                hop(int(step[1]), int(step[2]))
+        else:
+            with jax.named_scope(step + STAGES[step[0]]):
+                stages[STAGES[step[0]]](int(step[1]))
 
     for k in range(1, SLABS):
-        home(k).wait_recv()
+        arrive(home(k))
     out_copy = copy("out", 0, OS, OR, twin)
     for core in (0, 1):
         total = FIN[core]
@@ -294,19 +288,21 @@
     OS[...] = FIN[1 - c].astype(BF16)
     out_copy.start()
     out[:, pl.ds(mine, half)] = FIN[c].astype(BF16)
-    out_copy.wait_recv()
+    arrive(out_copy)
     out[:, pl.ds(other, half)] = OR[...]
 
-    pair_in(xh).wait_send()
+    pair_in(0).wait_send()
     weight_out.wait_send()
     out_copy.wait_send()
-    for n in range(4):
-        ring_down(n).wait_send()
-        ring_up(n).wait_send()
-
-    def drain(k, carry):
-        twin_in(k, c).wait_send()
+    for part in (0, 1):
+        for n in range(3):
+            ring_down(n, part).wait_send()
+            ring_up(n, part).wait_send()
+    ring_down(3, 0).wait_send()
+    ring_up(3, 1).wait_send()
+    for k in range(SLABS):
         for g in (0, 1):
+            twin_in(k, g, c).wait_send()
             far(k, g).wait_send()
             direct(k, g).wait_send()
             joint(k, g).wait_send()
@@ -316,14 +312,8 @@
             send.wait_send()
         twin_h(k, c).wait_send()
         halves(k).wait_send()
-
-        @pl.when(k > 0)
-        def _():
+        if k > 0:
             home(k).wait_send()
-
-        return carry
-
-    lax.fori_loop(0, SLABS, drain, 0)
 
 
 def per_device(tokens, gate_weight, up_weight, down_weight):

time: 131 us -> 102 us (0.78)
  Pallas kernels: 128 us -> 101 us
    pallas_call x1, Pallas kernels: 128 us -> 101 us  [per_device(): pl.pallas_call(kernel, out_shape=jax.ShapeDtypeStruct((rows, 2 * half), B...]
where the time goes in v2:
time: 102 us
  Pallas kernels  101 us (99%)
  local copies, waits for them, and re-layouts  1.57 us (2%)
    pallas_call x1, Pallas kernels, per_device(): pl.pallas_call(kernel, out_shape=jax.ShapeDtypeStruct((rows, 2 * half), B...  101 us

profile of v2, /device:TPU:1, one launch (start us, length us, event | category | flops | bytes accessed | tf_op | source)
XLA Modules:
  0.0 102.2 jit_solution(6181283870057610213)
XLA Ops:
  0.0 100.6 %block.1 = bf16[32,2048]{1,0:T(8,128)(2,1)} custom-call(bf16[32,2048]{1,0:T(8,128)(2,1)} %tokens.1, bf16[2048,896]{1,0:T(8,128)(2,1)} %gate_w.1, bf16[2048,896]{1,0:T(8,128)(2,1)} %up_w.1, bf16[896,2048]{1,0:T(8,128)(2,1)} %down_w.1), custom_call_target="tpu_custom_call" | custom-call | tf_op jit(solution)/shard_map/block/pallas_call | solution.py:324
  100.6 1.6 %copy.6 = bf16[32,2048]{1,0:T(8,128)(2,1)} copy(bf16[32,2048]{1,0:T(8,128)(2,1)} %block.1) | data formatting | bytes 262144

commit v3 on v2

--- a/solution.py
+++ b/solution.py
@@ -13,30 +13,30 @@
 MESH = pl.DeviceIdType.MESH
 BF16, F32 = jnp.bfloat16, jnp.float32
 SLABS = 8
-PLACE = (0, 1, 2, 3, 4, 5, 6, 7)
-STAGES = dict(g="gate_up", r="relay_y", a="add_y", s="activate", p="spread_y", t="to_twin", d="down", z="send_z")
+PLACE = (0, 1, 7, 2, 6, 3, 5, 4)
+STAGES = dict(g="gate_up", r="relay_y", a="add_y", s="activate", p="spread_y", t="to_twin", d="down", z="send_z", y="send_other_z")
 ORDER = (
-    "h00", "h01", "h10", "g0", "h11", "r0", "h20", "g1", "h21", "g7", "g6", "a0",
-    "h30", "h31", "r1", "g2", "g3", "a1", "h40", "s0", "r6", "r2", "r3", "g4",
-    "a6", "g5", "s1", "a3", "r4", "s6", "a2", "r5", "r7", "s3", "a4", "p6",
-    "s2", "a5", "p3", "s4", "p0", "t6", "a7", "p4", "p1", "t3", "s5", "d6",
-    "d3", "t0", "p5", "p2", "t4", "s7", "z6", "d4", "t5", "z3", "p7", "t2",
-    "d5", "z4", "t1", "d2", "t7", "d1", "z5", "d7", "d0", "z2", "z1", "z7",
-    "z0",
+    "h00", "h01", "h10", "g0", "h11", "r0", "h20", "g1", "h21", "g2", "a0", "g4",
+    "h31", "h30", "r1", "r2", "r4", "g5", "a1", "h40", "g6", "a4", "a2", "r5",
+    "g7", "r6", "g3", "s4", "a5", "r7", "s0", "a6", "p4", "s5", "r3", "a7",
+    "s6", "s2", "p5", "t4", "a3", "s7", "p6", "d4", "t5", "s3", "p7", "s1",
+    "p2", "d5", "t6", "z4", "y4", "p3", "d6", "p1", "t7", "z5", "t2", "d7",
+    "y5", "p0", "t3", "z6", "d3", "y6", "t1", "z7", "d2", "y7", "t0", "d1",
+    "z3", "d0", "y2", "y3", "z2", "y1", "z0", "z1", "y0",
 )
 FIRST_DOWN = next(step for step in ORDER if step[0] == "d")
 
 COPIES = dict(
     pair=1, up_ring=8, down_ring=8, twin_in=16,
     far=16, direct=16, joint=16, cross=8, cross_h=8, spread=24, twin_h=8,
-    half=8, home=8, out=1, weight=1,
+    half=16, home=16, own=1, weight=1,
 )
 BASE, TOTAL = {}, 0
 for _name, _count in COPIES.items():
     BASE[_name], TOTAL = TOTAL, TOTAL + _count
 
 
-def kernel(tokens, gate_w, up_w, down_w, out, T, GU, DW, PG, FS, FR, SS, SR, YB, XR, HB, PO, XS, XD, ZS, ZR, FIN, OS, OR, local, sent, got):
+def kernel(tokens, gate_w, up_w, down_w, out, T, GU, DW, PG, FS, FR, SS, SR, YB, XR, HB, PO, XS, XD, ZS, ZR, FIN, OTHER, local, sent, got):
     dp, mp = lax.axis_index("dp"), lax.axis_index("mp")
     z, xh, c = dp // 4, (dp // 2) & 1, dp & 1
     xl, y = mp // 4, mp & 3
@@ -51,8 +51,8 @@
     cross = device(xl_=1 - xl)
     y_up, y_down, y_far = (device(y_=(y + n) & 3) for n in (1, 3, 2))
 
-    def at_z(n):
-        return device(z_=(z + n) & 7)
+    def at_z(n, core=c):
+        return device(z_=(z + n) & 7, c_=core)
 
     mine = pl.multiple_of(c * half, half)
     other = pl.multiple_of((1 - c) * half, half)
@@ -66,7 +66,7 @@
         load.start()
 
     barrier = pltpu.get_barrier_semaphore()
-    friends = [twin, pair, cross, y_up, y_down, y_far] + [at_z(n) for n in range(1, 8)]
+    friends = [twin, pair, cross, y_up, y_down, y_far] + [at_z(n, core) for n in range(1, 8) for core in (c, 1 - c)]
     for friend in friends:
         pl.semaphore_signal(barrier, inc=1, device_id=friend, device_id_type=MESH)
     pl.semaphore_wait(barrier, len(friends))
@@ -172,11 +172,16 @@
         ref = HB.at[k, core]
         return copy("twin_h", k, ref, ref, twin)
 
-    def halves(k):
-        return copy("half", k, XS.at[k], XD.at[k], pair)
-
-    def home(k):
-        return copy("home", k, ZS.at[k], ZR.at[k], at_z(PLACE[k]))
+    def core_of(part):
+        return 1 - c if part else c
+
+    def halves(k, part):
+        return copy("half", 2 * k + part, XS.at[k, part], XD.at[k, part], pair)
+
+    def home(k, part):
+        return copy("home", 2 * k + part, ZS.at[k, part], ZR.at[k, part], at_z(PLACE[k], core_of(part)))
+
+    own_copy = copy("own", 0, FIN.at[1], OTHER, twin)
 
     def gate_up(k):
         n = PLACE[k]
@@ -251,23 +256,28 @@
             total = own + jnp.dot(HB[k, 1].reshape(128, width), DW[1, :, columns], preferred_element_type=F32)
             PO[k, :, :, columns] = total.reshape(4, 32, 256)
 
-        XS[k, 0] = PO[k, 1 - xh].astype(BF16)
-        XS[k, 1] = PO[k, 3 - xh].astype(BF16)
-        halves(k).start()
+        for part in (0, 1):
+            XS[k, part] = PO[k, 2 * core_of(part) + 1 - xh].astype(BF16)
+            halves(k, part).start()
+
+    def send_part(k, part):
+        arrive(halves(k, part))
+        total = PO[k, 2 * core_of(part) + xh] + XD[k, part].astype(F32)
+        if k == 0:
+            FIN[part] = total
+            if part == 1:
+                own_copy.start()
+        else:
+            ZS[k, part] = total.astype(BF16)
+            home(k, part).start()
 
     def send_z(k):
-        arrive(halves(k))
-        totals = [PO[k, 2 * core + xh] + XD[k, core].astype(F32) for core in (0, 1)]
-
-        if k == 0:
-            FIN[0] = totals[0]
-            FIN[1] = totals[1]
-        else:
-            ZS[k, 0] = totals[0].astype(BF16)
-            ZS[k, 1] = totals[1].astype(BF16)
-            home(k).start()
-
-    stages = dict(gate_up=gate_up, relay_y=relay_y, add_y=add_y, activate=activate, spread_y=spread_y, to_twin=to_twin, down=down, send_z=send_z)
+        send_part(k, 0)
+
+    def send_other_z(k):
+        send_part(k, 1)
+
+    stages = dict(gate_up=gate_up, relay_y=relay_y, add_y=add_y, activate=activate, spread_y=spread_y, to_twin=to_twin, down=down, send_z=send_z, send_other_z=send_other_z)
 
     for step in ORDER:
         if step[0] == "h":
@@ -277,23 +287,9 @@
             with jax.named_scope(step + STAGES[step[0]]):
                 stages[STAGES[step[0]]](int(step[1]))
 
-    for k in range(1, SLABS):
-        arrive(home(k))
-    out_copy = copy("out", 0, OS, OR, twin)
-    for core in (0, 1):
-        total = FIN[core]
-        for k in range(1, SLABS):
-            total += ZR[k, core].astype(F32)
-        FIN[core] = total
-    OS[...] = FIN[1 - c].astype(BF16)
-    out_copy.start()
-    out[:, pl.ds(mine, half)] = FIN[c].astype(BF16)
-    arrive(out_copy)
-    out[:, pl.ds(other, half)] = OR[...]
-
     pair_in(0).wait_send()
     weight_out.wait_send()
-    out_copy.wait_send()
+    own_copy.wait_send()
     for part in (0, 1):
         for n in range(3):
             ring_down(n, part).wait_send()
@@ -311,9 +307,21 @@
         for send in spreads(k):
             send.wait_send()
         twin_h(k, c).wait_send()
-        halves(k).wait_send()
-        if k > 0:
-            home(k).wait_send()
+        for part in (0, 1):
+            halves(k, part).wait_send()
+
+    arrive(own_copy)
+    for k in range(1, SLABS):
+        arrive(home(k, 0))
+        arrive(home(k, 1))
+    for part, (first, columns) in enumerate(((FIN.at[0], mine), (OTHER, other))):
+        total = first[...]
+        for k in range(1, SLABS):
+            total += ZR[k, part].astype(F32)
+        out[:, pl.ds(columns, half)] = total.astype(BF16)
+    for k in range(1, SLABS):
+        home(k, 0).wait_send()
+        home(k, 1).wait_send()
 
 
 def per_device(tokens, gate_weight, up_weight, down_weight):
@@ -344,8 +352,7 @@
             pltpu.VMEM((8, 2, 32, half), BF16),
             pltpu.VMEM((8, 2, 32, half), BF16),
             pltpu.VMEM((2, 32, half), F32),
-            pltpu.VMEM((32, half), BF16),
-            pltpu.VMEM((32, half), BF16),
+            pltpu.VMEM((32, half), F32),
             dma((4,)),
             dma((TOTAL,)),
             dma((TOTAL,)),

time: 102 us -> 100 us (0.980)
  Pallas kernels: 101 us -> 98.3 us
    pallas_call x1, Pallas kernels: 101 us -> 98.3 us  [per_device(): pl.pallas_call(kernel, out_shape=jax.ShapeDtypeStruct((rows, 2 * half), B...]
where the time goes in v3:
time: 100 us; the launch traced here: 99.9 us
  Pallas kernels  98.3 us (98%)
  local copies, waits for them, and re-layouts  1.57 us (2%)
    pallas_call x1, Pallas kernels, per_device(): pl.pallas_call(kernel, out_shape=jax.ShapeDtypeStruct((rows, 2 * half), B...  98.3 us

profile of v3, /device:TPU:1, one launch (start us, length us, event | category | flops | bytes accessed | tf_op | source)
XLA Modules:
  0.0 99.9 jit_solution(7758728380852129111)
XLA Ops:
  0.0 98.3 %block.1 = bf16[32,2048]{1,0:T(8,128)(2,1)} custom-call(bf16[32,2048]{1,0:T(8,128)(2,1)} %tokens.1, bf16[2048,896]{1,0:T(8,128)(2,1)} %gate_w.1, bf16[2048,896]{1,0:T(8,128)(2,1)} %up_w.1, bf16[896,2048]{1,0:T(8,128)(2,1)} %down_w.1), custom_call_target="tpu_custom_call" | custom-call | tf_op jit(solution)/shard_map/block/pallas_call | solution.py:332
  98.3 1.6 %copy.6 = bf16[32,2048]{1,0:T(8,128)(2,1)} copy(bf16[32,2048]{1,0:T(8,128)(2,1)} %block.1) | data formatting | bytes 262144

commit v4 on v3

--- a/solution.py
+++ b/solution.py
@@ -192,7 +192,7 @@
             loads[1].wait()
             loads[2].wait()
 
-        @pl.loop(0, 7)
+        @pl.loop(0, 7, unroll=True)
         def _(i):
             columns = pl.ds(pl.multiple_of(i * 256, 256), 256)
             rows = jnp.concatenate([T[s, (y + m) & 3] for m in (2, 1, 3, 0)], axis=0)
@@ -249,7 +249,7 @@
             loads[3].wait()
             arrive(weight_in)
 
-        @pl.loop(0, half // 256)
+        @pl.loop(0, half // 256, unroll=True)
         def _(i):
             columns = pl.ds(pl.multiple_of(i * 256, 256), 256)
             own = jnp.dot(HB[k, 0].reshape(128, width), DW[0, :, columns], preferred_element_type=F32)

time: 100 us -> 97.5 us (0.975)
  Pallas kernels: 98.3 us -> 95.9 us
    pallas_call x1, Pallas kernels: 98.3 us -> 95.9 us  [per_device(): pl.pallas_call(kernel, out_shape=jax.ShapeDtypeStruct((rows, 2 * half), B...]
where the time goes in v4:
time: 97.5 us
  Pallas kernels  95.9 us (98%)
  local copies, waits for them, and re-layouts  1.57 us (2%)
    pallas_call x1, Pallas kernels, per_device(): pl.pallas_call(kernel, out_shape=jax.ShapeDtypeStruct((rows, 2 * half), B...  95.9 us

profile of v4, /device:TPU:1, one launch (start us, length us, event | category | flops | bytes accessed | tf_op | source)
XLA Modules:
  0.0 97.5 jit_solution(15157761679220536576)
XLA Ops:
  0.0 95.9 %block.1 = bf16[32,2048]{1,0:T(8,128)(2,1)} custom-call(bf16[32,2048]{1,0:T(8,128)(2,1)} %tokens.1, bf16[2048,896]{1,0:T(8,128)(2,1)} %gate_w.1, bf16[2048,896]{1,0:T(8,128)(2,1)} %up_w.1, bf16[896,2048]{1,0:T(8,128)(2,1)} %down_w.1), custom_call_target="tpu_custom_call" | custom-call | tf_op jit(solution)/shard_map/block/pallas_call | solution.py:332
  95.9 1.6 %copy.6 = bf16[32,2048]{1,0:T(8,128)(2,1)} copy(bf16[32,2048]{1,0:T(8,128)(2,1)} %block.1) | data formatting | bytes 262144
